TPU v7x, 32 devices: a whole 2x2x4 slice. The times are simulated.
32 devices in a mesh: grp: 2 (over y), row: 4 (over z), col: 4 (over x, core).
Axes of the slice: x: 2, y: 2, z: 4, core: 2. Of those that a mesh axis runs over, the one named last changes fastest.
Arguments:
- z_spectra: float32 [32, 2, 2, 4096], P(('grp', 'row', 'col')), parts along dimension 0, may hold values from -6 to 6
- n_spectra: float32 [32, 2, 2, 4096], P(('grp', 'col', 'row')), parts along dimension 0, may hold values from -6 to 6
- z_flags: int32 [32, 2], P(('grp', 'row', 'col')), parts along dimension 0, may hold values 0 or 1
- n_flags: int32 [32, 2], P(('grp', 'col', 'row')), parts along dimension 0, may hold values 0 or 1
- pair_mask: int32 [32, 16], P(('grp', 'row'), 'col'), parts along dimension 0, may hold values 0 or 1
Outputs:
- stacks: float32 [32, 16, 512], P(('grp', 'row'), 'col'), parts along dimension 0
There are 2 independent parts, one for each index of `grp`. A program takes and returns all parts, laid end to end along the dimension named above; each array names one. Nothing has to cross between parts.
All inputs are finite; a program needn't handle non-finite values. No bound on the sum of `z_flags` or of `n_flags` or of `pair_mask` on one device may be relied on, other than what follows from the above.
Results may differ from a plain program's by a relative error of at most 0.0037.
Values sent between devices are 32-bit elements; how exact they have to be, the bound alone decides.
A program may use at most 64 MiB of HBM per device.

v0:
```python
import functools
import math

import jax
import jax.numpy as jnp
import numpy as np
from jax import lax
from jax.experimental import pallas as pl
from jax.experimental.pallas import tpu as pltpu
from jax.sharding import PartitionSpec as P

LAGS = 512
LANES = 128
MESH = pl.DeviceIdType.MESH
REACH = 3


def tables(bins):
    rows, blocks = bins // LANES, LAGS // LANES
    period = 2 * rows
    kt, short = np.arange(rows), np.arange(period)
    phi = 2 * np.pi * ((short[:, None] * kt[None, :]) % period) / period
    inner = np.block([[np.cos(phi), -np.sin(phi)], [np.sin(phi), np.cos(phi)]])
    lane, t0 = np.arange(LANES), np.arange(LANES)
    psi = np.pi * (t0[:, None] * lane[None, :]) / bins
    turn = np.stack([np.cos(psi), np.sin(psi)]).astype(np.float32)
    hop = np.arange(blocks) - blocks // 2
    chi = np.pi * ((LANES * hop[:, None] * lane[None, :]) % (2 * bins)) / bins
    outer = np.concatenate([np.cos(chi), -np.sin(chi)], 1).astype(np.float32)
    high = outer.astype(jnp.bfloat16)
    low = (outer - high.astype(np.float32)).astype(jnp.bfloat16)
    return inner.astype(jnp.bfloat16), turn, np.concatenate([high, low], 0)


def kernel(R, C, reach, z_hbm, n_hbm, zf_hbm, nf_hbm, mask_hbm, inner_hbm, turn_hbm, outer_hbm, out_ref,
           z_buf, n_buf, zf_buf, nf_buf, mask_buf, inner, turn, outer,
           load_sem, z_send, z_recv, zf_send, zf_recv, right_send, left_send, n_recv,
           rf_send, lf_send, nf_recv, own_send, own_f_send, ready, turn_sem):
    row, col = lax.axis_index("row"), lax.axis_index("col")
    W = z_buf.shape[1]
    bin_rows = z_buf.shape[2] // 2
    period = inner.shape[0] // 2
    blocks = outer.shape[0] // 2

    loads = [
        pltpu.make_async_copy(n_hbm.at[0], n_buf.at[row], load_sem.at[0]),
        pltpu.make_async_copy(z_hbm.at[0], z_buf.at[col], load_sem.at[1]),
        pltpu.make_async_copy(nf_hbm, nf_buf.at[row], load_sem.at[2]),
        pltpu.make_async_copy(zf_hbm, zf_buf.at[col], load_sem.at[3]),
        pltpu.make_async_copy(mask_hbm, mask_buf, load_sem.at[4]),
        pltpu.make_async_copy(inner_hbm, inner, load_sem.at[5]),
        pltpu.make_async_copy(turn_hbm, turn, load_sem.at[6]),
        pltpu.make_async_copy(outer_hbm, outer, load_sem.at[7]),
    ]
    for load in loads:
        load.start()

    has_left, has_right = row > 0, row < R - 1
    barrier = pltpu.get_barrier_semaphore()

    def there(hop):
        return (row + hop < R) if hop > 0 else (row + hop >= 0)

    for hop in (-1, 1):
        @pl.when(there(hop))
        def _():
            pl.semaphore_signal(barrier, inc=1, device_id={"row": row + hop}, device_id_type=MESH)

    for step in range(1, C):
        pl.semaphore_signal(barrier, inc=1, device_id={"col": lax.rem(col + step, C)}, device_id_type=MESH)
    pl.semaphore_wait(barrier, C - 1 + jnp.where(has_left, 1, 0) + jnp.where(has_right, 1, 0))

    def tell(hop):
        far = abs(hop) + 1
        back = -1 if hop > 0 else 1
        if far <= reach:
            @pl.when(there(hop) & there(back))
            def _():
                pl.semaphore_signal(ready.at[int(hop < 0), far], inc=1,
                                    device_id={"row": row + back}, device_id_type=MESH)

    def learn(hop):
        @pl.when(there(hop))
        def _():
            pl.semaphore_wait(ready.at[int(hop < 0), abs(hop)], 1)

    tell(1)
    tell(-1)

    def spectrum(owner, w, send, to):
        return pltpu.make_async_remote_copy(
            n_buf.at[owner, w], n_buf.at[owner, w], send.at[owner, w], n_recv.at[owner, w],
            device_id={"row": to}, device_id_type=MESH)

    def flag(owner, send, to):
        return pltpu.make_async_remote_copy(
            nf_buf.at[owner], nf_buf.at[owner], send.at[owner], nf_recv.at[owner],
            device_id={"row": to}, device_id_type=MESH)

    def z_copy(owner, w, to):
        return pltpu.make_async_remote_copy(
            z_buf.at[owner, w], z_buf.at[owner, w], z_send.at[to, w], z_recv.at[owner, w],
            device_id={"col": to}, device_id_type=MESH)

    def zf_copy(owner, to):
        return pltpu.make_async_remote_copy(
            zf_buf.at[owner], zf_buf.at[owner], zf_send.at[to], zf_recv.at[owner],
            device_id={"col": to}, device_id_type=MESH)

    def own_copy(hop, w):
        side, far = int(hop < 0), abs(hop) - 1
        return pltpu.make_async_remote_copy(
            n_buf.at[row, w], n_buf.at[row, w], own_send.at[side, far, w], n_recv.at[row, w],
            device_id={"row": row + hop}, device_id_type=MESH)

    def own_flag(hop):
        side, far = int(hop < 0), abs(hop) - 1
        return pltpu.make_async_remote_copy(
            nf_buf.at[row], nf_buf.at[row], own_f_send.at[side, far], nf_recv.at[row],
            device_id={"row": row + hop}, device_id_type=MESH)

    pairs = C % 2 == 0
    first = (lax.rem(col, 2) == 0) if pairs else (col >= 0)

    def send_own(hop):
        @pl.when(there(hop))
        def _():
            own_flag(hop).start()
            for w in range(W):
                own_copy(hop, w).start()

    for hop in range(2, reach + 1):
        learn(-hop)
        tell(-hop)
    loads[2].wait()
    loads[0].wait()
    @pl.when(first)
    def _():
        for hop in range(reach, 0, -1):
            send_own(-hop)

    send_own(1)
    loads[3].wait()
    loads[1].wait()
    for step in range(1, C):
        zf_copy(col, lax.rem(col + step, C)).start()
    for w in range(W):
        for step in range(1, C):
            z_copy(col, w, lax.rem(col + step, C)).start()
    @pl.when(first)
    def _():
        for hop in range(1, reach + 1):
            @pl.when((row == hop) | ((row > hop) & (hop == reach)))
            def _():
                for w in range(W):
                    own_copy(-hop, w).wait_send()

        if pairs:
            pl.semaphore_signal(turn_sem, inc=1, device_id={"col": lax.rem(col + 1, C)}, device_id_type=MESH)

    @pl.when(jnp.logical_not(first))
    def _():
        send_own(-1)
        held = row == R - 1

        @pl.when(held)
        def _():
            pl.semaphore_wait(turn_sem, 1)

        for hop in range(reach, 1, -1):
            send_own(-hop)

        @pl.when(jnp.logical_not(held))
        def _():
            pl.semaphore_wait(turn_sem, 1)

    for hop in range(2, reach + 1):
        learn(hop)
        tell(hop)
        send_own(hop)
    for load in loads[4:]:
        load.wait()

    spot = lax.broadcasted_iota(jnp.int32, (bin_rows, LANES), 0) + lax.broadcasted_iota(
        jnp.int32, (bin_rows, LANES), 1)
    weight = jnp.where(spot == 0, 1.0, 2.0).astype(jnp.float32)

    def unit(owner):
        pairs = [(i, w) for i in range(C) for w in range(W)]
        n_real = [n_buf[owner, w, pl.ds(0, bin_rows, stride=2), :] * weight for w in range(W)]
        n_imag = [n_buf[owner, w, pl.ds(1, bin_rows, stride=2), :] * weight for w in range(W)]
        cross = []
        for i, w in pairs:
            z_real = z_buf[i, w, pl.ds(0, bin_rows, stride=2), :]
            z_imag = z_buf[i, w, pl.ds(1, bin_rows, stride=2), :]
            cross.append(jnp.concatenate(
                [z_real * n_real[w] + z_imag * n_imag[w], z_imag * n_real[w] - z_real * n_imag[w]], 0
            ).astype(jnp.bfloat16))
        short = jnp.dot(inner[...], jnp.concatenate(cross, 1), preferred_element_type=jnp.float32)
        turned = []
        for at in range(len(pairs)):
            real = short[:period, at * LANES:(at + 1) * LANES]
            imag = short[period:, at * LANES:(at + 1) * LANES]
            for part in range(LANES // period):
                cosine = turn[0, part * period:(part + 1) * period, :]
                sine = turn[1, part * period:(part + 1) * period, :]
                turned.append(jnp.concatenate(
                    [real * cosine - imag * sine, real * sine + imag * cosine], 1).astype(jnp.bfloat16))
        lags = lax.dot_general(outer[...], jnp.concatenate(turned, 0), (((1,), (1,)), ((), ())),
                               preferred_element_type=jnp.float32)
        lags = lags[:blocks] + lags[blocks:]
        n_flag = nf_buf[owner].astype(jnp.float32)
        mask = mask_buf[...].astype(jnp.float32)
        here = lax.broadcasted_iota(jnp.int32, mask.shape, 1) == owner
        kept = jnp.sum(jnp.where(here, mask, 0.0), axis=1, keepdims=True)
        for i in range(C):
            marks = zf_buf[i].astype(jnp.float32) * n_flag
            count = jnp.maximum(jnp.sum(marks, axis=1, keepdims=True), 1.0)
            gain = marks * kept[i:i + 1] / count
            total = jnp.zeros((blocks, LANES), jnp.float32)
            for w in range(W):
                at = i * W + w
                corr = lags[:, at * LANES:(at + 1) * LANES]
                power = jnp.sum(jnp.sum(corr * corr, axis=0, keepdims=True), axis=1, keepdims=True)
                spread = jnp.sqrt(power / LAGS + 1e-05)
                total = total + corr * (gain[:, w:w + 1] / spread)
            out_ref[pl.ds(i * blocks * R + owner, blocks, stride=R), :] = total

    def arrive(owner, w, forward, send, f_send, to):
        if w == 0:
            flag(owner, f_send, to).wait_recv()
        spectrum(owner, w, send, to).wait_recv()
        if forward is False:
            return

        @pl.when(forward)
        def _():
            if w == 0:
                flag(owner, f_send, to).start()
            spectrum(owner, w, send, to).start()

    for step in range(1, C):
        zf_copy(lax.rem(col + C - step, C), lax.rem(col + step, C)).wait_recv()
    for w in range(W):
        for step in range(1, C):
            z_copy(lax.rem(col + C - step, C), w, lax.rem(col + step, C)).wait_recv()
    unit(row)

    def take(p):
        left = p <= row
        owner = jnp.where(left, row - p, p)
        if reach == R - 1:
            for w in range(W):
                arrive(owner, w, False, right_send, rf_send, lax.rem(row + 1, R))
        else:
            @pl.when(left)
            def _():
                for w in range(W):
                    arrive(owner, w, has_right & (p >= reach), right_send, rf_send, lax.rem(row + 1, R))

            @pl.when(p > row)
            def _():
                for w in range(W):
                    arrive(owner, w, has_left & (p - row >= reach), left_send, lf_send,
                           lax.rem(row + R - 1, R))
        unit(owner)

    if R <= 4:
        for p in range(1, R):
            take(p)
    else:
        pl.loop(1, R)(take)

    hops = [sign * hop for hop in range(1, reach + 1) for sign in (1, -1)]
    for hop in hops:
        @pl.when(there(hop))
        def _():
            own_flag(hop).wait_send()
            if hop > 0:
                for w in range(W):
                    own_copy(hop, w).wait_send()
            else:
                waited = first & ((row == -hop) | ((row > -hop) & (-hop == reach)))

                @pl.when(jnp.logical_not(waited))
                def _():
                    for w in range(W):
                        own_copy(hop, w).wait_send()

    for step in range(1, C):
        zf_copy(col, lax.rem(col + step, C)).wait_send()
        for w in range(W):
            z_copy(col, w, lax.rem(col + step, C)).wait_send()

    if reach == R - 1:
        return

    @pl.loop(0, R)
    def _(owner):
        @pl.when(has_right & (owner <= row - reach))
        def _():
            flag(owner, rf_send, lax.rem(row + 1, R)).wait_send()
            for w in range(W):
                spectrum(owner, w, right_send, lax.rem(row + 1, R)).wait_send()

        @pl.when(has_left & (owner >= row + reach))
        def _():
            flag(owner, lf_send, lax.rem(row + R - 1, R)).wait_send()
            for w in range(W):
                spectrum(owner, w, left_send, lax.rem(row + R - 1, R)).wait_send()


def body(R, C, z_spectra, n_spectra, z_flags, n_flags, pair_mask):
    windows, bins = z_spectra.shape[1], z_spectra.shape[3]
    rows, blocks = bins // LANES, LAGS // LANES
    inner, turn, outer = tables(bins)

    def interleave(x):
        return x.reshape(1, windows, 2, rows, LANES).transpose(0, 1, 3, 2, 4).reshape(
            1, windows, 2 * rows, LANES)

    reach = min(REACH, R - 1)
    DMA = pltpu.SemaphoreType.DMA
    out = pl.pallas_call(
        functools.partial(kernel, R, C, reach),
        out_shape=pltpu.VMEM((C * blocks * R, LANES), jnp.float32),
        in_specs=[pl.BlockSpec(memory_space=pl.ANY)] * 8,
        out_specs=pl.BlockSpec(memory_space=pltpu.VMEM),
        scratch_shapes=[
            pltpu.VMEM((C, windows, 2 * rows, LANES), jnp.float32),
            pltpu.VMEM((R, windows, 2 * rows, LANES), jnp.float32),
            pltpu.VMEM((C, 1, windows), jnp.int32),
            pltpu.VMEM((R, 1, windows), jnp.int32),
            pltpu.VMEM(pair_mask.shape, jnp.int32),
            pltpu.VMEM(inner.shape, jnp.bfloat16),
            pltpu.VMEM(turn.shape, jnp.float32),
            pltpu.VMEM(outer.shape, jnp.bfloat16),
            DMA((8,)),
            DMA((C, windows)), DMA((C, windows)), DMA((C,)), DMA((C,)),
            DMA((R, windows)), DMA((R, windows)), DMA((R, windows)),
            DMA((R,)), DMA((R,)), DMA((R,)),
            DMA((2, reach, windows)), DMA((2, reach)), pltpu.SemaphoreType.REGULAR((2, reach + 1)),
            pltpu.SemaphoreType.REGULAR,
        ],
        compiler_params=pltpu.CompilerParams(collective_id=0, has_side_effects=True),
        name="correlate",
    )(interleave(z_spectra), interleave(n_spectra), z_flags, n_flags, pair_mask,
      jnp.asarray(inner), jnp.asarray(turn), jnp.asarray(outer))
    return out.reshape(C, blocks, R, LANES).transpose(0, 2, 1, 3).reshape(C, R, LAGS)


def solution(mesh):
    placed = (
        P(("grp", "row", "col"), None, None, None),
        P(("grp", "col", "row"), None, None, None),
        P(("grp", "row", "col"), None),
        P(("grp", "col", "row"), None),
        P(("grp", "row"), "col"),
    )
    return jax.shard_map(
        functools.partial(body, mesh.shape["row"], mesh.shape["col"]), mesh=mesh,
        in_specs=placed, out_specs=P(("grp", "row"), "col", None), check_vma=False,
    )
```

profile of v0, /device:TPU:1, one launch (start us, length us, event | category | flops | bytes accessed | tf_op | source)
XLA Modules:
  0.0 13.5 jit_solution(16198298582000661381)
XLA Ops:
  0.0 12.9 %correlate.1 = f32[64,128]{1,0:T(8,128)S(1)} custom-call(f32[1,2,64,128]{3,2,1,0:T(8,128)} %bitcast.16, f32[1,2,64,128]{3,2,1,0:T(8,128)} %bitcast.17, s32[1,2]{1,0:T(1,128)} %zf_hbm.1, s32[1,2]{1,0:T(1,128)} %nf_hbm.1, s32[4,4]{1,0:T(4,128)} %mask_hbm.1, bf16[128,64]{1,0:T(8,128)(2,1)} %constant.6.clone.inner_hbm, f32[2,128,128]{2,1,0:T(8,128)} %constant.7.clone.turn_hbm, ...), custom_call_target="tpu_custom_call" | custom-call | tf_op jit(solution)/shard_map/correlate/pallas_call | solution.py:324
  12.9 0.6 %copy.13 = f32[4,4,512]{2,1,0:T(4,128)} copy(f32[4,4,512]{2,1,0:T(4,128)S(1)} %bitcast.15) | data formatting | bytes 65536
where the time goes:
time: 13.6 us; the launch traced here: 13.5 us
  Pallas kernels  12.9 us (95%)
  local copies, waits for them, and re-layouts  0.62 us (5%)
    pallas_call x1, Pallas kernels, body(): pl.pallas_call(functools.partial(kernel, R, C, reach), out_shape=pltpu.VM...  12.9 us
    unnamed x1, local copies, waits for them, and re-layouts  0.62 us

commit v1 on v0

v1 whole, which is shorter than its diff:
```python
import functools
import math

import jax
import jax.numpy as jnp
import numpy as np
from jax import lax
from jax.experimental import pallas as pl
from jax.experimental.pallas import tpu as pltpu
from jax.sharding import PartitionSpec as P

LAGS = 512
LANES = 128
MESH = pl.DeviceIdType.MESH
REACH = 3


def tables(bins):
    rows = bins // LANES
    period = 2 * rows
    blocks = LAGS // period
    kt, short = np.arange(rows), np.arange(period)
    phi = 2 * np.pi * ((short[:, None] * kt[None, :]) % period) / period
    inner = np.block([[np.cos(phi), -np.sin(phi)], [np.sin(phi), np.cos(phi)]])
    lane = np.arange(LANES)
    psi = np.pi * (short[:, None] * lane[None, :]) / bins
    turn = np.stack([np.cos(psi), np.sin(psi)]).astype(np.float32)
    split = LANES // period
    hop = np.arange(blocks).reshape(-1, split).T.reshape(-1) - blocks // 2
    chi = np.pi * ((period * hop[:, None] * lane[None, :]) % (2 * bins)) / bins
    outer = np.concatenate([np.cos(chi), -np.sin(chi)], 1).astype(np.float32)
    high = outer.astype(jnp.bfloat16)
    low = (outer - high.astype(np.float32)).astype(jnp.bfloat16)
    return inner.astype(jnp.bfloat16), turn, np.concatenate([high, low], 0)


def kernel(R, C, reach, z_hbm, n_hbm, zf_hbm, nf_hbm, mask_hbm, inner_hbm, turn_hbm, outer_hbm, out_ref,
           z_buf, n_buf, zf_buf, nf_buf, mask_buf, inner, turn, outer,
           load_sem, z_send, z_recv, zf_send, zf_recv, right_send, left_send, n_recv,
           rf_send, lf_send, nf_recv, own_send, own_f_send, row_ready, col_ready, turn_sem, go_sem):
    row, col = lax.axis_index("row"), lax.axis_index("col")
    W = z_buf.shape[1]
    bin_rows = z_buf.shape[2] // 2
    period = inner.shape[0] // 2
    blocks = outer.shape[0] // 2

    loads = [
        pltpu.make_async_copy(n_hbm.at[0], n_buf.at[row], load_sem.at[0]),
        pltpu.make_async_copy(z_hbm.at[0], z_buf.at[col], load_sem.at[1]),
        pltpu.make_async_copy(nf_hbm, nf_buf.at[row], load_sem.at[2]),
        pltpu.make_async_copy(zf_hbm, zf_buf.at[col], load_sem.at[3]),
        pltpu.make_async_copy(mask_hbm, mask_buf, load_sem.at[4]),
        pltpu.make_async_copy(inner_hbm, inner, load_sem.at[5]),
        pltpu.make_async_copy(turn_hbm, turn, load_sem.at[6]),
        pltpu.make_async_copy(outer_hbm, outer, load_sem.at[7]),
    ]
    for load in loads:
        load.start()

    has_left, has_right = row > 0, row < R - 1
    barrier = pltpu.get_barrier_semaphore()
    hops = range(1, reach + 1)

    def there(hop):
        return (row + hop < R) if hop > 0 else (row + hop >= 0)

    for hop in hops:
        @pl.when(there(hop))
        def _():
            pl.semaphore_signal(barrier, inc=1, device_id={"row": row + hop}, device_id_type=MESH)

    for step in range(1, C):
        @pl.when(col + step < C)
        def _():
            pl.semaphore_signal(barrier, inc=1, device_id={"col": col + step}, device_id_type=MESH)

    ahead = col + jnp.minimum(row, reach)

    @pl.when(ahead > 0)
    def _():
        pl.semaphore_wait(barrier, ahead)

    for hop in hops:
        @pl.when(there(-hop))
        def _():
            pl.semaphore_signal(row_ready.at[hop], inc=1, device_id={"row": row - hop}, device_id_type=MESH)

    for step in range(1, C):
        @pl.when(col >= step)
        def _():
            pl.semaphore_signal(col_ready.at[step], inc=1, device_id={"col": col - step}, device_id_type=MESH)

    def spectrum(owner, w, send, to):
        return pltpu.make_async_remote_copy(
            n_buf.at[owner, w], n_buf.at[owner, w], send.at[owner, w], n_recv.at[owner, w],
            device_id={"row": to}, device_id_type=MESH)

    def flag(owner, send, to):
        return pltpu.make_async_remote_copy(
            nf_buf.at[owner], nf_buf.at[owner], send.at[owner], nf_recv.at[owner],
            device_id={"row": to}, device_id_type=MESH)

    def z_copy(owner, w, to):
        return pltpu.make_async_remote_copy(
            z_buf.at[owner, w], z_buf.at[owner, w], z_send.at[owner, to, w], z_recv.at[owner, w],
            device_id={"col": to}, device_id_type=MESH)

    def zf_copy(owner, to):
        return pltpu.make_async_remote_copy(
            zf_buf.at[owner], zf_buf.at[owner], zf_send.at[to], zf_recv.at[owner],
            device_id={"col": to}, device_id_type=MESH)

    def own_copy(hop, w):
        side, far = int(hop < 0), abs(hop) - 1
        return pltpu.make_async_remote_copy(
            n_buf.at[row, w], n_buf.at[row, w], own_send.at[side, far, w], n_recv.at[row, w],
            device_id={"row": row + hop}, device_id_type=MESH)

    def own_flag(hop):
        side, far = int(hop < 0), abs(hop) - 1
        return pltpu.make_async_remote_copy(
            nf_buf.at[row], nf_buf.at[row], own_f_send.at[side, far], nf_recv.at[row],
            device_id={"row": row + hop}, device_id_type=MESH)

    def send_own(hop):
        @pl.when(there(hop))
        def _():
            if hop > 0:
                pl.semaphore_wait(row_ready.at[hop], 1)
            own_flag(hop).start()

        @pl.when(there(hop) & sends(hop))
        def _():
            for w in range(W):
                own_copy(hop, w).start()

    relayed = C % 2 == 0
    partner = col + 1 - 2 * lax.rem(col, 2)

    loads[2].wait()
    loads[0].wait()
    far0 = jnp.minimum(row, reach)
    second = (row < 0)

    odd = lax.rem(col, 2) == 1
    relay_left = odd
    relay_right = (row >= 0)

    far = jnp.where(relay_left & (far0 == 2), 1, far0)

    def sends(hop):
        if hop == -2:
            return jnp.logical_not(relay_left)
        if hop == 2:
            return jnp.logical_not(relay_right)
        return row >= 0

    def left(hop):
        for w in range(W):
            own_copy(-hop, w).start()

    for hop in range(1, reach + 1):
        @pl.when(there(-hop))
        def _():
            own_flag(-hop).start()

        @pl.when((far == hop) & jnp.logical_not(second) & sends(-hop))
        def _():
            left(hop)

    @pl.when(second)
    def _():
        left(1)

    def own_done(hop):
        for w in range(W):
            own_copy(-hop, w).wait_send()

    def rest():
        @pl.when(second)
        def _():
            pl.semaphore_wait(turn_sem, 1)
            for hop in range(reach, 1, -1):
                @pl.when(sends(-hop))
                def _():
                    left(hop)

        @pl.when(jnp.logical_not(second))
        def _():
            if False:
                @pl.when((far > 1) & (row < R - 1))
                def _():
                    pl.semaphore_wait(go_sem, 1)
            for hop in range(reach - 1, 0, -1):
                @pl.when((far > hop) & sends(-hop))
                def _():
                    left(hop)

    def turns():
        last = row == R - 1
        if True:
            @pl.when(row < 0)
            def _():
                own_done(reach)
                pl.semaphore_signal(turn_sem, inc=1, device_id={"col": partner}, device_id_type=MESH)
        if False:
            @pl.when(last)
            def _():
                if True:
                    @pl.when(lax.rem(col, 2) == 1)
                    def _():
                        own_done(reach)
                else:
                    own_done(reach)
                pl.semaphore_signal(go_sem, inc=1, device_id={"row": row - 1}, device_id_type=MESH)

    loads[3].wait()
    loads[1].wait()
    def each_col(fn):
        for step in range(1, C):
            to = lax.rem(col + step, C)
            fn(step, to)

    def wanted(to):
        return ((lax.rem(to, 2) == 1) | (to == partner)) if relayed else (col >= 0)

    def send_z(step, to):
        @pl.when(wanted(to))
        def _():
            @pl.when(to > col)
            def _():
                pl.semaphore_wait(col_ready.at[step], 1)

            for w in range(W):
                z_copy(col, w, to).start()

    def send_zf(step, to):
        @pl.when((to > col) & jnp.logical_not(wanted(to)))
        def _():
            pl.semaphore_wait(col_ready.at[step], 1)

        zf_copy(col, to).start()

    def z_all():
        each_col(send_z)
        each_col(send_zf)

    def n_right():
        for hop in range(1, reach + 1):
            send_own(hop)
    turns()
    z_all()
    rest()
    n_right()
    from_left = relay_right & has_left & has_right
    from_right = relay_left & has_left & has_right

    @pl.when(from_right)
    def _():
        for w in range(W):
            spectrum(row + 1, w, left_send, row - 1).wait_recv()
            spectrum(row + 1, w, left_send, row - 1).start()

    @pl.when(from_left)
    def _():
        for w in range(W):
            spectrum(row - 1, w, right_send, row + 1).wait_recv()
            spectrum(row - 1, w, right_send, row + 1).start()

    if relayed:
        @pl.when(odd)
        def _():
            for step in range(1, C):
                owner = lax.rem(col + step, C)

                @pl.when(owner != partner)
                def _():
                    for w in range(W):
                        z_copy(owner, w, partner).wait_recv()
                        z_copy(owner, w, partner).start()

    for load in loads[4:]:
        load.wait()

    spot = lax.broadcasted_iota(jnp.int32, (bin_rows, LANES), 0) + lax.broadcasted_iota(
        jnp.int32, (bin_rows, LANES), 1)
    weight = jnp.where(spot == 0, 1.0, 2.0).astype(jnp.float32)

    split = LANES // period
    lines = blocks // split
    groups = C // split
    lane_side = lax.broadcasted_iota(jnp.int32, (blocks, LANES), 1) // period
    line_side = lax.broadcasted_iota(jnp.int32, (blocks, LANES), 0) // lines

    def spread_out(rows):
        picked = jnp.zeros((blocks, LANES), jnp.float32) + rows[0]
        for h in range(1, split):
            picked = jnp.where(line_side == h, rows[h], picked)
        return picked

    def gains(owner):
        n_flag = nf_buf[owner].astype(jnp.float32)
        mask = mask_buf[...].astype(jnp.float32)
        here = lax.broadcasted_iota(jnp.int32, mask.shape, 1) == owner
        kept = jnp.sum(jnp.where(here, mask, 0.0), axis=1, keepdims=True)
        each = []
        for i in range(C):
            marks = zf_buf[i].astype(jnp.float32) * n_flag
            count = jnp.maximum(jnp.sum(marks, axis=1, keepdims=True), 1.0)
            each.append(marks * kept[i:i + 1] / count)
        return [[spread_out([each[g * split + h][:, w:w + 1] for h in range(split)]) for g in range(groups)]
                for w in range(W)]

    def correlate(owner):
        cross = []
        for w in range(W):
            n_real = n_buf[owner, w, pl.ds(0, bin_rows, stride=2), :] * weight
            n_imag = n_buf[owner, w, pl.ds(1, bin_rows, stride=2), :] * weight
            for i in range(C):
                z_real = z_buf[i, w, pl.ds(0, bin_rows, stride=2), :]
                z_imag = z_buf[i, w, pl.ds(1, bin_rows, stride=2), :]
                cross.append(jnp.concatenate(
                    [z_real * n_real + z_imag * n_imag, z_imag * n_real - z_real * n_imag], 0
                ).astype(jnp.bfloat16))
        short = jnp.dot(inner[...], jnp.concatenate(cross, 1), preferred_element_type=jnp.float32)
        turned = []
        for at in range(W * C):
            real = short[:period, at * LANES:(at + 1) * LANES]
            imag = short[period:, at * LANES:(at + 1) * LANES]
            turned.append(jnp.concatenate(
                [real * turn[0] - imag * turn[1], real * turn[1] + imag * turn[0]], 1).astype(jnp.bfloat16))
        lags = lax.dot_general(outer[...], jnp.concatenate(turned, 0), (((1,), (1,)), ((), ())),
                               preferred_element_type=jnp.float32)
        lags = lags[:blocks] + lags[blocks:]
        return [[lags[:, (w * groups + g) * LANES:(w * groups + g + 1) * LANES] for g in range(groups)]
                for w in range(W)]

    def normal(corr, gain):
        power = jnp.sum(corr * corr, axis=0, keepdims=True)
        whole = spread_out([jnp.sum(jnp.where(lane_side[:1] == h, power, 0.0), axis=1, keepdims=True)
                            for h in range(split)])
        laid = corr
        for by in range(1, split):
            moved = pltpu.roll(pltpu.roll(corr, by * period, 1), (split - by) * lines, 0)
            laid = jnp.where(lax.rem(lane_side - line_side + split, split) == by, moved, laid)
        return laid * (gain * lax.rsqrt(whole / LAGS + 1e-05))

    def finish(owner, corrs, gain):
        for g in range(groups):
            total = normal(corrs[0][g], gain[0][g])
            for w in range(1, W):
                total = total + normal(corrs[w][g], gain[w][g])
            for h in range(split):
                i = g * split + h
                out_ref[pl.ds(i * lines * R + owner, lines, stride=R), :] = total[h * lines:(h + 1) * lines]

    def unit(owner, gain):
        finish(owner, correlate(owner), gain)

    def arrive(owner, w, forward, send, f_send, to):
        if w == 0:
            flag(owner, f_send, to).wait_recv()
        spectrum(owner, w, send, to).wait_recv()
        if forward is False:
            return

        @pl.when(forward)
        def _():
            if w == 0:
                flag(owner, f_send, to).start()
            spectrum(owner, w, send, to).start()

    for step in range(1, C):
        owner = lax.rem(col + step, C)
        zf_copy(owner, col).wait_recv()

        @pl.when(jnp.logical_not(odd) | (owner == partner) if relayed else col >= 0)
        def _():
            for w in range(W):
                z_copy(owner, w, col).wait_recv()

    def source(p):
        return jnp.where(p <= row, row - p, p)

    def receive(p):
        left = p <= row
        owner = source(p)
        if reach == R - 1:
            got = (from_left & (owner == row - 1)) | (from_right & (owner == row + 1))

            @pl.when(jnp.logical_not(got))
            def _():
                for w in range(W):
                    spectrum(owner, w, right_send, lax.rem(row + 1, R)).wait_recv()
        else:
            @pl.when(left)
            def _():
                for w in range(W):
                    arrive(owner, w, has_right & (p >= reach), right_send, rf_send, lax.rem(row + 1, R))

            @pl.when(p > row)
            def _():
                for w in range(W):
                    arrive(owner, w, has_left & (p - row >= reach), left_send, lf_send,
                           lax.rem(row + R - 1, R))

    def batch(ps):
        owners = [row if p == 0 else source(p) for p in ps]
        gain = [gains(owner) for owner in owners]
        for p in ps:
            if p > 0:
                receive(p)
        corrs = [correlate(owner) for owner in owners]
        for owner, corr, g in zip(owners, corrs, gain):
            finish(owner, corr, g)

    if R <= 4:
        for p in range(1, R):
            flag(source(p), rf_send, lax.rem(row + 1, R)).wait_recv()
        for ps in [[0, 1], [2, 3]]:
            batch([p for p in ps if p < R])
    else:
        unit(row, gains(row))

        @pl.loop(1, R)
        def _(p):
            receive(p)
            unit(source(p), gains(source(p)))


    for hop in hops:
        for side in (hop, -hop):
            @pl.when(there(side))
            def _():
                own_flag(side).wait_send()

            done = (row < 0) if side > 0 else (row < 0)
            @pl.when(there(side) & jnp.logical_not(done) & sends(side))
            def _():
                for w in range(W):
                    own_copy(side, w).wait_send()

    for step in range(1, C):
        to = lax.rem(col + step, C)
        zf_copy(col, to).wait_send()
        @pl.when(wanted(to))
        def _():
            for w in range(W):
                z_copy(col, w, to).wait_send()

        if relayed:
            @pl.when(odd & (to != partner))
            def _():
                for w in range(W):
                    z_copy(to, w, partner).wait_send()

    @pl.when(from_right)
    def _():
        for w in range(W):
            spectrum(row + 1, w, left_send, row - 1).wait_send()

    @pl.when(from_left)
    def _():
        for w in range(W):
            spectrum(row - 1, w, right_send, row + 1).wait_send()

    if reach == R - 1:
        return

    @pl.loop(0, R)
    def _(owner):
        @pl.when(has_right & (owner <= row - reach))
        def _():
            flag(owner, rf_send, lax.rem(row + 1, R)).wait_send()
            for w in range(W):
                spectrum(owner, w, right_send, lax.rem(row + 1, R)).wait_send()

        @pl.when(has_left & (owner >= row + reach))
        def _():
            flag(owner, lf_send, lax.rem(row + R - 1, R)).wait_send()
            for w in range(W):
                spectrum(owner, w, left_send, lax.rem(row + R - 1, R)).wait_send()


def body(R, C, z_spectra, n_spectra, z_flags, n_flags, pair_mask):
    windows, bins = z_spectra.shape[1], z_spectra.shape[3]
    rows, blocks = bins // LANES, LAGS // LANES
    inner, turn, outer = tables(bins)

    def interleave(x):
        return x.reshape(1, windows, 2, rows, LANES).transpose(0, 1, 3, 2, 4).reshape(
            1, windows, 2 * rows, LANES)

    reach = min(REACH, R - 1)
    DMA = pltpu.SemaphoreType.DMA
    out = pl.pallas_call(
        functools.partial(kernel, R, C, reach),
        out_shape=pltpu.VMEM((C * blocks * R, LANES), jnp.float32),
        in_specs=[pl.BlockSpec(memory_space=pl.ANY)] * 8,
        out_specs=pl.BlockSpec(memory_space=pltpu.VMEM),
        scratch_shapes=[
            pltpu.VMEM((C, windows, 2 * rows, LANES), jnp.float32),
            pltpu.VMEM((R, windows, 2 * rows, LANES), jnp.float32),
            pltpu.VMEM((C, 1, windows), jnp.int32),
            pltpu.VMEM((R, 1, windows), jnp.int32),
            pltpu.VMEM(pair_mask.shape, jnp.int32),
            pltpu.VMEM(inner.shape, jnp.bfloat16),
            pltpu.VMEM(turn.shape, jnp.float32),
            pltpu.VMEM(outer.shape, jnp.bfloat16),
            DMA((8,)),
            DMA((C, C, windows)), DMA((C, windows)), DMA((C,)), DMA((C,)),
            DMA((R, windows)), DMA((R, windows)), DMA((R, windows)),
            DMA((R,)), DMA((R,)), DMA((R,)),
            DMA((2, reach, windows)), DMA((2, reach)),
            pltpu.SemaphoreType.REGULAR((reach + 1,)), pltpu.SemaphoreType.REGULAR((C,)),
            pltpu.SemaphoreType.REGULAR, pltpu.SemaphoreType.REGULAR,
        ],
        compiler_params=pltpu.CompilerParams(collective_id=0, has_side_effects=True),
        name="correlate",
    )(interleave(z_spectra), interleave(n_spectra), z_flags, n_flags, pair_mask,
      jnp.asarray(inner), jnp.asarray(turn), jnp.asarray(outer))
    return out.reshape(C, blocks, R, LANES).transpose(0, 2, 1, 3).reshape(C, R, LAGS)


def solution(mesh):
    placed = (
        P(("grp", "row", "col"), None, None, None),
        P(("grp", "col", "row"), None, None, None),
        P(("grp", "row", "col"), None),
        P(("grp", "col", "row"), None),
        P(("grp", "row"), "col"),
    )
    return jax.shard_map(
        functools.partial(body, mesh.shape["row"], mesh.shape["col"]), mesh=mesh,
        in_specs=placed, out_specs=P(("grp", "row"), "col", None), check_vma=False,
    )
```

time: 13.6 us -> 11.3 us (0.83)
  Pallas kernels: 12.9 us -> 10.5 us
    pallas_call x1, Pallas kernels: 12.9 us -> 10.5 us  [body(): pl.pallas_call(functools.partial(kernel, R, C, reach), out_shape=pltpu.VM...]
where the time goes in v1:
time: 11.3 us; the launch traced here: 11.1 us
  Pallas kernels  10.5 us (93%)
  local copies, waits for them, and re-layouts  0.62 us (5%)
    pallas_call x1, Pallas kernels, body(): pl.pallas_call(functools.partial(kernel, R, C, reach), out_shape=pltpu.VM...  10.5 us
    unnamed x1, local copies, waits for them, and re-layouts  0.62 us

profile of v1, /device:TPU:1, one launch (start us, length us, event | category | flops | bytes accessed | tf_op | source)
XLA Modules:
  0.0 11.1 jit_solution(17073733561848091108)
XLA Ops:
  0.0 10.5 %correlate.1 = f32[64,128]{1,0:T(8,128)S(1)} custom-call(f32[1,2,64,128]{3,2,1,0:T(8,128)} %bitcast.16, f32[1,2,64,128]{3,2,1,0:T(8,128)} %bitcast.17, s32[1,2]{1,0:T(1,128)} %zf_hbm.1, s32[1,2]{1,0:T(1,128)} %nf_hbm.1, s32[4,4]{1,0:T(4,128)} %mask_hbm.1, bf16[128,64]{1,0:T(8,128)(2,1)} %constant.6.clone.inner_hbm, f32[2,64,128]{2,1,0:T(8,128)} %constant.7.clone.turn_hbm, ...), custom_call_target="tpu_custom_call" | custom-call | tf_op jit(solution)/shard_map/correlate/pallas_call | solution.py:496
  10.5 0.6 %copy.13 = f32[4,4,512]{2,1,0:T(4,128)} copy(f32[4,4,512]{2,1,0:T(4,128)S(1)} %bitcast.15) | data formatting | bytes 65536

commit v2 on v0

--- a/solution.py
+++ b/solution.py
@@ -16,6 +16,353 @@
 
 
 def tables(bins):
+    rows = bins // LANES
+    period = 2 * rows
+    blocks, split = LAGS // period, LANES // period
+    kt, short, lane = np.arange(rows), np.arange(period), np.arange(LANES)
+    phi = 2 * np.pi * ((short[:, None] * kt[None, :]) % period) / period
+    inner = np.block([[np.cos(phi), -np.sin(phi)], [np.sin(phi), np.cos(phi)]])
+    psi = np.pi * (short[:, None] * lane[None, :]) / bins
+    hop = np.arange(blocks).reshape(-1, split).T.reshape(-1) - blocks // 2
+    chi = np.pi * ((period * hop[:, None] * lane[None, :]) % (2 * bins)) / bins
+    outer = np.stack([np.cos(chi), -np.sin(chi)]).astype(np.float32)
+    high = outer.astype(jnp.bfloat16).astype(np.float32)
+    low = (outer - high).astype(jnp.bfloat16).astype(np.float32)
+    wide = np.pad(inner, ((0, 0), (0, LANES - inner.shape[1])))
+    parts = [wide, np.cos(psi), np.sin(psi), high[0], low[0], high[1], low[1]]
+    return np.concatenate(parts, 0).astype(np.float32)
+
+
+def kernel(R, C, z_hbm, n_hbm, zf_hbm, nf_hbm, mask_hbm, table_hbm, out_ref,
+           z_buf, n_buf, zf_buf, nf_buf, mask_buf, table,
+           load_sem, n_recv, z_recv, flag_recv, sent, row_ready, col_ready):
+    row, col = lax.axis_index("row"), lax.axis_index("col")
+    W = z_buf.shape[1]
+    bin_rows = z_buf.shape[2] // 2
+    period = 2 * bin_rows
+    blocks = LAGS // period
+    odd = lax.rem(col, 2) == 1
+    partner = col + 1 - 2 * lax.rem(col, 2)
+
+    n_load = pltpu.make_async_copy(n_hbm.at[0], n_buf.at[row], n_recv.at[row, 0])
+    z_load = pltpu.make_async_copy(z_hbm.at[0], z_buf.at[col], z_recv.at[col])
+    nf_load = pltpu.make_async_copy(nf_hbm, nf_buf.at[row], load_sem.at[0])
+    zf_load = pltpu.make_async_copy(zf_hbm, zf_buf.at[col], load_sem.at[1])
+    mask_load = pltpu.make_async_copy(mask_hbm, mask_buf, load_sem.at[2])
+    table_load = pltpu.make_async_copy(table_hbm, table, load_sem.at[3])
+    for load in (n_load, z_load, nf_load, zf_load, mask_load, table_load):
+        load.start()
+
+    def row_there(hop):
+        return (row + hop < R) & (row + hop >= 0)
+
+    barrier = pltpu.get_barrier_semaphore()
+    for hop in range(1, R):
+        @pl.when(row_there(hop))
+        def _():
+            pl.semaphore_signal(barrier, inc=1, device_id={"row": row + hop}, device_id_type=MESH)
+
+    for step in range(1, C):
+        @pl.when(col + step < C)
+        def _():
+            pl.semaphore_signal(barrier, inc=1, device_id={"col": col + step}, device_id_type=MESH)
+
+    @pl.when(row + col > 0)
+    def _():
+        pl.semaphore_wait(barrier, row + col)
+
+    for hop in range(1, R):
+        @pl.when(row_there(-hop))
+        def _():
+            pl.semaphore_signal(row_ready.at[hop - 1], inc=1, device_id={"row": row - hop}, device_id_type=MESH)
+
+    for step in range(1, C):
+        @pl.when(col >= step)
+        def _():
+            pl.semaphore_signal(col_ready.at[step - 1], inc=1, device_id={"col": col - step}, device_id_type=MESH)
+
+    def spectrum(owner, w, to):
+        return pltpu.make_async_remote_copy(
+            n_buf.at[owner, w], n_buf.at[owner, w], sent.at[0], n_recv.at[owner, w],
+            device_id={"row": to}, device_id_type=MESH)
+
+    def n_flag(to):
+        return pltpu.make_async_remote_copy(
+            nf_buf.at[row], nf_buf.at[row], sent.at[1], flag_recv.at[0],
+            device_id={"row": to}, device_id_type=MESH)
+
+    def z_copy(owner, to):
+        return pltpu.make_async_remote_copy(
+            z_buf.at[owner], z_buf.at[owner], sent.at[2], z_recv.at[owner],
+            device_id={"col": to}, device_id_type=MESH)
+
+    def z_flag(to):
+        return pltpu.make_async_remote_copy(
+            zf_buf.at[col], zf_buf.at[col], sent.at[3], flag_recv.at[1],
+            device_id={"col": to}, device_id_type=MESH)
+
+    relay_left, relay_right = odd, row >= 0
+
+    def direct(hop):
+        if hop == -2:
+            return row_there(hop) & jnp.logical_not(relay_left)
+        if hop == 2:
+            return row_there(hop) & jnp.logical_not(relay_right)
+        return row_there(hop)
+
+    def send_n(hop):
+        for w in range(W):
+            spectrum(row, w, row + hop).start()
+
+    inside = (row > 0) & (row < R - 1)
+    from_left, from_right = inside & relay_right, inside & relay_left
+
+    def relay_n(owner, to):
+        for w in range(W):
+            spectrum(owner, w, to).wait_recv()
+            spectrum(owner, w, to).start()
+
+    n_load.wait()
+    nf_load.wait()
+    for hop in range(1, R):
+        @pl.when(row_there(-hop))
+        def _():
+            n_flag(row - hop).start()
+
+    lead = jnp.where((row == 2) & relay_left, 1, row)
+    for hop in range(1, R):
+        @pl.when(lead == hop)
+        def _():
+            send_n(-hop)
+
+    z_load.wait()
+    zf_load.wait()
+
+    for step in range(1, C):
+        to = lax.rem(col + step, C)
+        wide = (lax.rem(to, 2) == 1) | (to == partner)
+
+        @pl.when(wide)
+        def _():
+            @pl.when(to > col)
+            def _():
+                pl.semaphore_wait(col_ready.at[step - 1], 1)
+
+            z_copy(col, to).start()
+
+    for step in range(1, C):
+        to = lax.rem(col + step, C)
+        wide = (lax.rem(to, 2) == 1) | (to == partner)
+
+        @pl.when(jnp.logical_not(wide) & (to > col))
+        def _():
+            pl.semaphore_wait(col_ready.at[step - 1], 1)
+
+        z_flag(to).start()
+
+    for hop in range(R - 1, 0, -1):
+        @pl.when((lead > hop) & direct(-hop))
+        def _():
+            send_n(-hop)
+
+    for hop in range(1, R):
+        @pl.when(row_there(hop))
+        def _():
+            pl.semaphore_wait(row_ready.at[hop - 1], 1)
+            n_flag(row + hop).start()
+
+        @pl.when(direct(hop))
+        def _():
+            send_n(hop)
+
+    @pl.when(from_right)
+    def _():
+        relay_n(row + 1, row - 1)
+
+    @pl.when(from_left)
+    def _():
+        relay_n(row - 1, row + 1)
+
+    @pl.when(odd)
+    def _():
+        for step in range(1, C):
+            owner = lax.rem(col + step, C)
+
+            @pl.when(owner != partner)
+            def _():
+                z_copy(owner, partner).wait_recv()
+                z_copy(owner, partner).start()
+
+    mask_load.wait()
+    table_load.wait()
+    spot = lax.broadcasted_iota(jnp.int32, (bin_rows, LANES), 0) + lax.broadcasted_iota(
+        jnp.int32, (bin_rows, LANES), 1)
+    weight = jnp.where(spot == 0, 1.0, 2.0).astype(jnp.float32)
+    split = LANES // period
+    lines = blocks // split
+    groups = C // split
+    lane_side = lax.broadcasted_iota(jnp.int32, (blocks, LANES), 1) // period
+    line_side = lax.broadcasted_iota(jnp.int32, (blocks, LANES), 0) // lines
+
+    def spread_out(rows):
+        picked = jnp.zeros((blocks, LANES), jnp.float32) + rows[0]
+        for h in range(1, split):
+            picked = jnp.where(line_side == h, rows[h], picked)
+        return picked
+
+    def gains(owner):
+        passed = nf_buf[owner].astype(jnp.float32)
+        mask = mask_buf[...].astype(jnp.float32)
+        here = lax.broadcasted_iota(jnp.int32, mask.shape, 1) == owner
+        kept = jnp.sum(jnp.where(here, mask, 0.0), axis=1, keepdims=True)
+        each = []
+        for i in range(C):
+            marks = zf_buf[i].astype(jnp.float32) * passed
+            count = jnp.maximum(jnp.sum(marks, axis=1, keepdims=True), 1.0)
+            each.append(marks * kept[i:i + 1] / count)
+        return [[spread_out([each[g * split + h][:, w:w + 1] for h in range(split)]) for g in range(groups)]
+                for w in range(W)]
+
+    def correlate(owner):
+        inner = table[:2 * period, :period].astype(jnp.bfloat16)
+        turn = table[2 * period:3 * period, :], table[3 * period:4 * period, :]
+        outer = jnp.concatenate([table[4 * period:4 * period + 2 * blocks, :], table[4 * period + 2 * blocks:, :]], 1)
+        outer = outer.astype(jnp.bfloat16)
+        cross = []
+        for w in range(W):
+            n_real = n_buf[owner, w, pl.ds(0, bin_rows, stride=2), :] * weight
+            n_imag = n_buf[owner, w, pl.ds(1, bin_rows, stride=2), :] * weight
+            for i in range(C):
+                z_real = z_buf[i, w, pl.ds(0, bin_rows, stride=2), :]
+                z_imag = z_buf[i, w, pl.ds(1, bin_rows, stride=2), :]
+                cross.append(jnp.concatenate(
+                    [z_real * n_real + z_imag * n_imag, z_imag * n_real - z_real * n_imag], 0
+                ).astype(jnp.bfloat16))
+        short = jnp.dot(inner, jnp.concatenate(cross, 1), preferred_element_type=jnp.float32)
+        turned = []
+        for at in range(W * C):
+            real = short[:period, at * LANES:(at + 1) * LANES]
+            imag = short[period:, at * LANES:(at + 1) * LANES]
+            turned.append(jnp.concatenate(
+                [real * turn[0] - imag * turn[1], real * turn[1] + imag * turn[0]], 1).astype(jnp.bfloat16))
+        lags = lax.dot_general(outer, jnp.concatenate(turned, 0), (((1,), (1,)), ((), ())),
+                               preferred_element_type=jnp.float32)
+        lags = lags[:blocks] + lags[blocks:]
+        return [[lags[:, (w * groups + g) * LANES:(w * groups + g + 1) * LANES] for g in range(groups)]
+                for w in range(W)]
+
+    def normal(corr, gain):
+        power = jnp.sum(corr * corr, axis=0, keepdims=True)
+        whole = spread_out([jnp.sum(jnp.where(lane_side[:1] == h, power, 0.0), axis=1, keepdims=True)
+                            for h in range(split)])
+        laid = corr
+        for by in range(1, split):
+            moved = pltpu.roll(pltpu.roll(corr, by * period, 1), (split - by) * lines, 0)
+            laid = jnp.where(lax.rem(lane_side - line_side + split, split) == by, moved, laid)
+        return laid * (gain * lax.rsqrt(whole / LAGS + 1e-05))
+
+    def finish(owner, corrs, gain):
+        for g in range(groups):
+            total = normal(corrs[0][g], gain[0][g])
+            for w in range(1, W):
+                total = total + normal(corrs[w][g], gain[w][g])
+            for h in range(split):
+                i = g * split + h
+                out_ref[pl.ds(i * lines * R + owner, lines, stride=R), :] = total[h * lines:(h + 1) * lines]
+
+    def pick(p):
+        ranks = sorted(range(1, R), key=lambda far: (far == 2, far))
+        owner = row * 0
+        for at in range(R):
+            owners = [at + side * far for far in ranks for side in (-1, 1) if 0 <= at + side * far < R]
+            owner = jnp.where(row == at, owners[p - 1], owner)
+        return owner
+
+    def receive(owner):
+        got = (from_left & (owner == row - 1)) | (from_right & (owner == row + 1))
+
+        @pl.when(jnp.logical_not(got))
+        def _():
+            for w in range(W):
+                spectrum(owner, w, row).wait_recv()
+
+    for step in range(1, C):
+        owner = lax.rem(col + step, C)
+
+        @pl.when(jnp.logical_not(odd) | (owner == partner))
+        def _():
+            z_copy(owner, col).wait_recv()
+
+    flags = zf_buf.at[pl.ds(0, C - 1)]
+    pltpu.make_async_copy(flags, flags, flag_recv.at[1]).wait()
+    flags = nf_buf.at[pl.ds(0, R - 1)]
+    pltpu.make_async_copy(flags, flags, flag_recv.at[0]).wait()
+    owners = [row] + [pick(p) for p in range(1, R)]
+    gain = None
+    for batch in ((0, 1), (2,), (3,)):
+        batch = [p for p in batch if p < R]
+        for p in batch:
+            if p > 0:
+                receive(owners[p])
+        if gain is None:
+            gain = [gains(owner) for owner in owners]
+        corrs = [correlate(owners[p]) for p in batch]
+        for p, corr in zip(batch, corrs):
+            finish(owners[p], corr, gain[p])
+
+    def drain(ref, count, most, sem):
+        for k in range(1, most + 1):
+            @pl.when(count == k)
+            def _():
+                some = ref.at[pl.ds(0, k)]
+                pltpu.make_async_copy(some, some, sem).wait()
+
+    def ones(*flags):
+        return sum(jnp.where(flag, 1, 0) for flag in flags)
+
+    own = ones(*[direct(side * hop) for hop in range(1, R) for side in (1, -1)])
+    drain(n_buf, own + ones(from_left, from_right), R, sent.at[0])
+    drain(nf_buf, row * 0 + R - 1, R - 1, sent.at[1])
+    drain(z_buf, jnp.where(odd, C // 2 + C - 2, C // 2), C, sent.at[2])
+    drain(zf_buf, row * 0 + C - 1, C - 1, sent.at[3])
+
+
+def body(R, C, z_spectra, n_spectra, z_flags, n_flags, pair_mask):
+    windows, bins = z_spectra.shape[1], z_spectra.shape[3]
+    rows = bins // LANES
+    blocks, split = LAGS // (2 * rows), LANES // (2 * rows)
+    if R > 4 or C != 4 or C % split:
+        return far_body(R, C, z_spectra, n_spectra, z_flags, n_flags, pair_mask)
+    table = jnp.asarray(tables(bins))
+
+    def interleave(x):
+        return x.reshape(1, windows, 2, rows, LANES).transpose(0, 1, 3, 2, 4).reshape(
+            1, windows, 2 * rows, LANES)
+
+    DMA, REGULAR = pltpu.SemaphoreType.DMA, pltpu.SemaphoreType.REGULAR
+    lines = blocks // split
+    out = pl.pallas_call(
+        functools.partial(kernel, R, C),
+        out_shape=pltpu.VMEM((C * lines * R, LANES), jnp.float32),
+        in_specs=[pl.BlockSpec(memory_space=pl.ANY)] * 6,
+        out_specs=pl.BlockSpec(memory_space=pltpu.VMEM),
+        scratch_shapes=[
+            pltpu.VMEM((C, windows, 2 * rows, LANES), jnp.float32),
+            pltpu.VMEM((R, windows, 2 * rows, LANES), jnp.float32),
+            pltpu.VMEM((C, 1, windows), jnp.int32),
+            pltpu.VMEM((R, 1, windows), jnp.int32),
+            pltpu.VMEM(pair_mask.shape, jnp.int32),
+            pltpu.VMEM(table.shape, jnp.float32),
+            DMA((4,)), DMA((R, windows)), DMA((C,)), DMA((2,)), DMA((4,)),
+            REGULAR((R - 1,)), REGULAR((C - 1,)),
+        ],
+        compiler_params=pltpu.CompilerParams(collective_id=0, has_side_effects=True),
+        name="correlate",
+    )(interleave(z_spectra), interleave(n_spectra), z_flags, n_flags, pair_mask, table)
+    return out.reshape(C, lines, R, LANES).transpose(0, 2, 1, 3).reshape(C, R, LAGS)
+
+
+def far_tables(bins):
     rows, blocks = bins // LANES, LAGS // LANES
     period = 2 * rows
     kt, short = np.arange(rows), np.arange(period)
@@ -32,7 +379,7 @@
     return inner.astype(jnp.bfloat16), turn, np.concatenate([high, low], 0)
 
 
-def kernel(R, C, reach, z_hbm, n_hbm, zf_hbm, nf_hbm, mask_hbm, inner_hbm, turn_hbm, outer_hbm, out_ref,
+def far_kernel(R, C, reach, z_hbm, n_hbm, zf_hbm, nf_hbm, mask_hbm, inner_hbm, turn_hbm, outer_hbm, out_ref,
            z_buf, n_buf, zf_buf, nf_buf, mask_buf, inner, turn, outer,
            load_sem, z_send, z_recv, zf_send, zf_recv, right_send, left_send, n_recv,
            rf_send, lf_send, nf_recv, own_send, own_f_send, ready, turn_sem):
@@ -310,10 +657,10 @@
                 spectrum(owner, w, left_send, lax.rem(row + R - 1, R)).wait_send()
 
 
-def body(R, C, z_spectra, n_spectra, z_flags, n_flags, pair_mask):
+def far_body(R, C, z_spectra, n_spectra, z_flags, n_flags, pair_mask):
     windows, bins = z_spectra.shape[1], z_spectra.shape[3]
     rows, blocks = bins // LANES, LAGS // LANES
-    inner, turn, outer = tables(bins)
+    inner, turn, outer = far_tables(bins)
 
     def interleave(x):
         return x.reshape(1, windows, 2, rows, LANES).transpose(0, 1, 3, 2, 4).reshape(
@@ -322,7 +669,7 @@
     reach = min(REACH, R - 1)
     DMA = pltpu.SemaphoreType.DMA
     out = pl.pallas_call(
-        functools.partial(kernel, R, C, reach),
+        functools.partial(far_kernel, R, C, reach),
         out_shape=pltpu.VMEM((C * blocks * R, LANES), jnp.float32),
         in_specs=[pl.BlockSpec(memory_space=pl.ANY)] * 8,
         out_specs=pl.BlockSpec(memory_space=pltpu.VMEM),

time: 13.6 us -> 10.5 us (0.77)
  the two profiles are of different devices: /device:TPU:1 before, /device:TPU:0 now
where the time goes in v2:
time: 10.5 us; the launch traced here: 10.3 us
  Pallas kernels  9.71 us (92%)
  local copies, waits for them, and re-layouts  0.62 us (6%)
    pallas_call x1, Pallas kernels, body(): pl.pallas_call(functools.partial(kernel, R, C), out_shape=pltpu.VMEM((C *...  9.71 us
    unnamed x1, local copies, waits for them, and re-layouts  0.62 us

profile of v2, /device:TPU:0, one launch (start us, length us, event | category | flops | bytes accessed | tf_op | source)
XLA Modules:
  0.0 10.3 jit_solution(597781648727308190)
XLA Ops:
  0.0 9.7 %correlate.1 = f32[64,128]{1,0:T(8,128)S(1)} custom-call(f32[1,2,64,128]{3,2,1,0:T(8,128)} %bitcast.16, f32[1,2,64,128]{3,2,1,0:T(8,128)} %bitcast.17, s32[1,2]{1,0:T(1,128)} %zf_hbm.1, s32[1,2]{1,0:T(1,128)} %nf_hbm.1, s32[4,4]{1,0:T(4,128)} %mask_hbm.1, f32[288,128]{1,0:T(8,128)} %constant.2.clone.table_hbm), custom_call_target="tpu_custom_call" | custom-call | tf_op jit(solution)/shard_map/correlate/pallas_call | solution.py:344
  9.7 0.6 %copy.11 = f32[4,4,512]{2,1,0:T(4,128)} copy(f32[4,4,512]{2,1,0:T(4,128)S(1)} %bitcast.15) | data formatting | bytes 65536

commit v3 on v2

--- a/solution.py
+++ b/solution.py
@@ -13,6 +13,19 @@
 LANES = 128
 MESH = pl.DeviceIdType.MESH
 REACH = 3
+SENDS = (
+    ((0, 1, 3), (0, 3, 5)),
+    ((0, 1, 3), (0, 3, 5)),
+    ((1, 0, 0), (1, 2, 3), (0, 2, 6)),
+    ((1, 0, 0), (1, 2, 3), (2, 0, 6), (0, 2, 6)),
+    ((2, 0, 0), (2, 1, 2), (2, 3, 3), (1, 3, 6)),
+    ((2, 1, 0), (2, 3, 3), (3, 1, 6), (1, 3, 6)),
+    ((3, 0, 0), (3, 1, 2), (3, 2, 2)),
+    ((3, 0, 0), (3, 2, 2)),
+)
+TAKES = ((1, 2, 3), (1, 2, 3), (0, 2, 3), (0, 2, 3), (1, 3, 0), (1, 3, 0), (2, 0, 1), (2, 0, 1))
+BATCHES = ((0, 1), (2, 3))
+GAIN_AT = 1
 
 
 def tables(bins):
@@ -34,24 +47,26 @@
 
 
 def kernel(R, C, z_hbm, n_hbm, zf_hbm, nf_hbm, mask_hbm, table_hbm, out_ref,
-           z_buf, n_buf, zf_buf, nf_buf, mask_buf, table,
-           load_sem, n_recv, z_recv, flag_recv, sent, row_ready, col_ready):
+           held, flags, mask_buf, table, n_recv, z_recv, flag_recv, sent, row_ready, col_ready):
     row, col = lax.axis_index("row"), lax.axis_index("col")
-    W = z_buf.shape[1]
-    bin_rows = z_buf.shape[2] // 2
+    W = held.shape[1]
+    bin_rows = held.shape[2] // 2
     period = 2 * bin_rows
     blocks = LAGS // period
     odd = lax.rem(col, 2) == 1
     partner = col + 1 - 2 * lax.rem(col, 2)
-
-    n_load = pltpu.make_async_copy(n_hbm.at[0], n_buf.at[row], n_recv.at[row, 0])
-    z_load = pltpu.make_async_copy(z_hbm.at[0], z_buf.at[col], z_recv.at[col])
-    nf_load = pltpu.make_async_copy(nf_hbm, nf_buf.at[row], load_sem.at[0])
-    zf_load = pltpu.make_async_copy(zf_hbm, zf_buf.at[col], load_sem.at[1])
-    mask_load = pltpu.make_async_copy(mask_hbm, mask_buf, load_sem.at[2])
-    table_load = pltpu.make_async_copy(table_hbm, table, load_sem.at[3])
-    for load in (n_load, z_load, nf_load, zf_load, mask_load, table_load):
-        load.start()
+    place = 2 * row + lax.rem(col, 2)
+
+    def wait_all(ref, count, sem):
+        some = ref.at[pl.ds(0, count)]
+        pltpu.make_async_copy(some, some, sem).wait()
+
+    n_load = pltpu.make_async_copy(n_hbm.at[0], held.at[row], n_recv.at[row, 0])
+    z_load = pltpu.make_async_copy(z_hbm.at[0], held.at[R + col], z_recv.at[col])
+    n_load.start()
+    pltpu.make_async_copy(nf_hbm, flags.at[row], sent.at[1]).start()
+    pltpu.make_async_copy(zf_hbm, flags.at[R + col], sent.at[1]).start()
+    z_load.start()
 
     def row_there(hop):
         return (row + hop < R) & (row + hop >= 0)
@@ -79,120 +94,93 @@
     for step in range(1, C):
         @pl.when(col >= step)
         def _():
-            pl.semaphore_signal(col_ready.at[step - 1], inc=1, device_id={"col": col - step}, device_id_type=MESH)
+            pl.semaphore_signal(col_ready, inc=1, device_id={"col": col - step}, device_id_type=MESH)
 
     def spectrum(owner, w, to):
         return pltpu.make_async_remote_copy(
-            n_buf.at[owner, w], n_buf.at[owner, w], sent.at[0], n_recv.at[owner, w],
+            held.at[owner, w], held.at[owner, w], sent.at[0], n_recv.at[owner, w],
             device_id={"row": to}, device_id_type=MESH)
 
-    def n_flag(to):
-        return pltpu.make_async_remote_copy(
-            nf_buf.at[row], nf_buf.at[row], sent.at[1], flag_recv.at[0],
-            device_id={"row": to}, device_id_type=MESH)
-
     def z_copy(owner, to):
         return pltpu.make_async_remote_copy(
-            z_buf.at[owner], z_buf.at[owner], sent.at[2], z_recv.at[owner],
+            held.at[R + owner], held.at[R + owner], sent.at[0], z_recv.at[owner],
             device_id={"col": to}, device_id_type=MESH)
 
-    def z_flag(to):
-        return pltpu.make_async_remote_copy(
-            zf_buf.at[col], zf_buf.at[col], sent.at[3], flag_recv.at[1],
-            device_id={"col": to}, device_id_type=MESH)
-
-    relay_left, relay_right = odd, row >= 0
-
-    def direct(hop):
-        if hop == -2:
-            return row_there(hop) & jnp.logical_not(relay_left)
-        if hop == 2:
-            return row_there(hop) & jnp.logical_not(relay_right)
-        return row_there(hop)
-
-    def send_n(hop):
-        for w in range(W):
-            spectrum(row, w, row + hop).start()
-
-    inside = (row > 0) & (row < R - 1)
-    from_left, from_right = inside & relay_right, inside & relay_left
-
-    def relay_n(owner, to):
-        for w in range(W):
-            spectrum(owner, w, to).wait_recv()
-            spectrum(owner, w, to).start()
-
-    n_load.wait()
-    nf_load.wait()
+    def flag(slot, **to):
+        return pltpu.make_async_remote_copy(
+            flags.at[slot], flags.at[slot], sent.at[1], flag_recv, device_id=to, device_id_type=MESH)
+
+    def at(fn):
+        for here in range(2 * R):
+            @pl.when(place == here)
+            def _():
+                fn(here)
+
+    def step_sends(number):
+        def send(here):
+            for owner, to, when in SENDS[here]:
+                if when == number:
+                    for w in range(W):
+                        if owner != here // 2:
+                            spectrum(owner, w, to).wait_recv()
+                        spectrum(owner, w, to).start()
+        if any(when == number for sends in SENDS for _, _, when in sends):
+            at(send)
+
+    wait_all(flags, 2, sent.at[1])
     for hop in range(1, R):
         @pl.when(row_there(-hop))
         def _():
-            n_flag(row - hop).start()
-
-    lead = jnp.where((row == 2) & relay_left, 1, row)
-    for hop in range(1, R):
-        @pl.when(lead == hop)
-        def _():
-            send_n(-hop)
+            flag(row, row=row - hop).start()
+
+    n_load.wait()
+    mask_load = pltpu.make_async_copy(mask_hbm, mask_buf, n_recv.at[row, 0])
+    mask_load.start()
+    step_sends(0)
+
+    def send_z(step, ahead):
+        to = lax.rem(col + step, C)
+
+        @pl.when((to > col) == ahead)
+        def _():
+            @pl.when(jnp.logical_not(odd) | (lax.rem(to, 2) == 1) | (to == partner))
+            def _():
+                z_copy(col, to).start()
+
+            flag(R + col, col=to).start()
 
     z_load.wait()
-    zf_load.wait()
-
-    for step in range(1, C):
-        to = lax.rem(col + step, C)
-        wide = (lax.rem(to, 2) == 1) | (to == partner)
-
-        @pl.when(wide)
-        def _():
-            @pl.when(to > col)
-            def _():
-                pl.semaphore_wait(col_ready.at[step - 1], 1)
-
-            z_copy(col, to).start()
-
-    for step in range(1, C):
-        to = lax.rem(col + step, C)
-        wide = (lax.rem(to, 2) == 1) | (to == partner)
-
-        @pl.when(jnp.logical_not(wide) & (to > col))
-        def _():
-            pl.semaphore_wait(col_ready.at[step - 1], 1)
-
-        z_flag(to).start()
-
-    for hop in range(R - 1, 0, -1):
-        @pl.when((lead > hop) & direct(-hop))
-        def _():
-            send_n(-hop)
-
+    table_load = pltpu.make_async_copy(table_hbm, table, z_recv.at[col])
+    table_load.start()
+    for step in range(1, C):
+        send_z(step, False)
+    step_sends(1)
+
+    @pl.when(col < C - 1)
+    def _():
+        pl.semaphore_wait(col_ready, C - 1 - col)
+
+    for step in range(1, C):
+        send_z(step, True)
+    step_sends(2)
     for hop in range(1, R):
         @pl.when(row_there(hop))
         def _():
             pl.semaphore_wait(row_ready.at[hop - 1], 1)
-            n_flag(row + hop).start()
-
-        @pl.when(direct(hop))
-        def _():
-            send_n(hop)
-
-    @pl.when(from_right)
-    def _():
-        relay_n(row + 1, row - 1)
-
-    @pl.when(from_left)
-    def _():
-        relay_n(row - 1, row + 1)
+            flag(row, row=row + hop).start()
+
+        step_sends(2 + hop)
+
+    step_sends(R + 2)
 
     @pl.when(odd)
     def _():
-        for step in range(1, C):
+        for step in range(2, C, 2):
             owner = lax.rem(col + step, C)
-
-            @pl.when(owner != partner)
-            def _():
-                z_copy(owner, partner).wait_recv()
-                z_copy(owner, partner).start()
-
+            z_copy(owner, partner).wait_recv()
+            z_copy(owner, partner).start()
+
+    step_sends(R + 3)
     mask_load.wait()
     table_load.wait()
     spot = lax.broadcasted_iota(jnp.int32, (bin_rows, LANES), 0) + lax.broadcasted_iota(
@@ -211,13 +199,13 @@
         return picked
 
     def gains(owner):
-        passed = nf_buf[owner].astype(jnp.float32)
+        passed = flags[owner].astype(jnp.float32)
         mask = mask_buf[...].astype(jnp.float32)
         here = lax.broadcasted_iota(jnp.int32, mask.shape, 1) == owner
         kept = jnp.sum(jnp.where(here, mask, 0.0), axis=1, keepdims=True)
         each = []
         for i in range(C):
-            marks = zf_buf[i].astype(jnp.float32) * passed
+            marks = flags[R + i].astype(jnp.float32) * passed
             count = jnp.maximum(jnp.sum(marks, axis=1, keepdims=True), 1.0)
             each.append(marks * kept[i:i + 1] / count)
         return [[spread_out([each[g * split + h][:, w:w + 1] for h in range(split)]) for g in range(groups)]
@@ -230,11 +218,11 @@
         outer = outer.astype(jnp.bfloat16)
         cross = []
         for w in range(W):
-            n_real = n_buf[owner, w, pl.ds(0, bin_rows, stride=2), :] * weight
-            n_imag = n_buf[owner, w, pl.ds(1, bin_rows, stride=2), :] * weight
+            n_real = held[owner, w, pl.ds(0, bin_rows, stride=2), :] * weight
+            n_imag = held[owner, w, pl.ds(1, bin_rows, stride=2), :] * weight
             for i in range(C):
-                z_real = z_buf[i, w, pl.ds(0, bin_rows, stride=2), :]
-                z_imag = z_buf[i, w, pl.ds(1, bin_rows, stride=2), :]
+                z_real = held[R + i, w, pl.ds(0, bin_rows, stride=2), :]
+                z_imag = held[R + i, w, pl.ds(1, bin_rows, stride=2), :]
                 cross.append(jnp.concatenate(
                     [z_real * n_real + z_imag * n_imag, z_imag * n_real - z_real * n_imag], 0
                 ).astype(jnp.bfloat16))
@@ -251,7 +239,7 @@
         return [[lags[:, (w * groups + g) * LANES:(w * groups + g + 1) * LANES] for g in range(groups)]
                 for w in range(W)]
 
-    def normal(corr, gain):
+    def normal(corr):
         power = jnp.sum(corr * corr, axis=0, keepdims=True)
         whole = spread_out([jnp.sum(jnp.where(lane_side[:1] == h, power, 0.0), axis=1, keepdims=True)
                             for h in range(split)])
@@ -259,79 +247,64 @@
         for by in range(1, split):
             moved = pltpu.roll(pltpu.roll(corr, by * period, 1), (split - by) * lines, 0)
             laid = jnp.where(lax.rem(lane_side - line_side + split, split) == by, moved, laid)
-        return laid * (gain * lax.rsqrt(whole / LAGS + 1e-05))
-
-    def finish(owner, corrs, gain):
+        return laid * lax.rsqrt(whole / LAGS + 1e-05)
+
+    def finish(owner, units, gain):
         for g in range(groups):
-            total = normal(corrs[0][g], gain[0][g])
+            total = units[0][g] * gain[0][g]
             for w in range(1, W):
-                total = total + normal(corrs[w][g], gain[w][g])
+                total = total + units[w][g] * gain[w][g]
             for h in range(split):
                 i = g * split + h
                 out_ref[pl.ds(i * lines * R + owner, lines, stride=R), :] = total[h * lines:(h + 1) * lines]
 
     def pick(p):
-        ranks = sorted(range(1, R), key=lambda far: (far == 2, far))
         owner = row * 0
-        for at in range(R):
-            owners = [at + side * far for far in ranks for side in (-1, 1) if 0 <= at + side * far < R]
-            owner = jnp.where(row == at, owners[p - 1], owner)
+        for here in range(2 * R):
+            owner = jnp.where(place == here, TAKES[here][p - 1], owner)
         return owner
 
-    def receive(owner):
-        got = (from_left & (owner == row - 1)) | (from_right & (owner == row + 1))
-
-        @pl.when(jnp.logical_not(got))
-        def _():
-            for w in range(W):
-                spectrum(owner, w, row).wait_recv()
+    def receive(p):
+        def take(here):
+            owner = TAKES[here][p - 1]
+            if all(passed != owner for passed, _, _ in SENDS[here]):
+                for w in range(W):
+                    spectrum(owner, w, here // 2).wait_recv()
+        at(take)
 
     for step in range(1, C):
         owner = lax.rem(col + step, C)
 
-        @pl.when(jnp.logical_not(odd) | (owner == partner))
+        @pl.when(jnp.logical_not(odd & (lax.rem(owner, 2) == 1)))
         def _():
             z_copy(owner, col).wait_recv()
 
-    flags = zf_buf.at[pl.ds(0, C - 1)]
-    pltpu.make_async_copy(flags, flags, flag_recv.at[1]).wait()
-    flags = nf_buf.at[pl.ds(0, R - 1)]
-    pltpu.make_async_copy(flags, flags, flag_recv.at[0]).wait()
     owners = [row] + [pick(p) for p in range(1, R)]
-    gain = None
-    for batch in ((0, 1), (2,), (3,)):
-        batch = [p for p in batch if p < R]
+    done = []
+    for number, batch in enumerate(BATCHES):
+        if number == GAIN_AT:
+            wait_all(flags, R + C - 2, flag_recv)
+            gain = [gains(owner) for owner in owners]
         for p in batch:
             if p > 0:
-                receive(owners[p])
-        if gain is None:
-            gain = [gains(owner) for owner in owners]
+                receive(p)
         corrs = [correlate(owners[p]) for p in batch]
-        for p, corr in zip(batch, corrs):
-            finish(owners[p], corr, gain[p])
-
-    def drain(ref, count, most, sem):
-        for k in range(1, most + 1):
-            @pl.when(count == k)
-            def _():
-                some = ref.at[pl.ds(0, k)]
-                pltpu.make_async_copy(some, some, sem).wait()
-
-    def ones(*flags):
-        return sum(jnp.where(flag, 1, 0) for flag in flags)
-
-    own = ones(*[direct(side * hop) for hop in range(1, R) for side in (1, -1)])
-    drain(n_buf, own + ones(from_left, from_right), R, sent.at[0])
-    drain(nf_buf, row * 0 + R - 1, R - 1, sent.at[1])
-    drain(z_buf, jnp.where(odd, C // 2 + C - 2, C // 2), C, sent.at[2])
-    drain(zf_buf, row * 0 + C - 1, C - 1, sent.at[3])
+        done += [(p, [[normal(c) for c in part] for part in corr]) for p, corr in zip(batch, corrs)]
+    for p, units in done:
+        finish(owners[p], units, gain[p])
+
+    def finish_sends(here):
+        wait_all(held, len(SENDS[here]) + C - 1, sent.at[0])
+
+    at(finish_sends)
+    wait_all(flags, R + C - 2, sent.at[1])
 
 
 def body(R, C, z_spectra, n_spectra, z_flags, n_flags, pair_mask):
     windows, bins = z_spectra.shape[1], z_spectra.shape[3]
     rows = bins // LANES
     blocks, split = LAGS // (2 * rows), LANES // (2 * rows)
-    if R > 4 or C != 4 or C % split:
+    if 2 * R != len(SENDS) or C % 2 or C % split:
         return far_body(R, C, z_spectra, n_spectra, z_flags, n_flags, pair_mask)
     table = jnp.asarray(tables(bins))
 
@@ -347,14 +320,11 @@
         in_specs=[pl.BlockSpec(memory_space=pl.ANY)] * 6,
         out_specs=pl.BlockSpec(memory_space=pltpu.VMEM),
         scratch_shapes=[
-            pltpu.VMEM((C, windows, 2 * rows, LANES), jnp.float32),
-            pltpu.VMEM((R, windows, 2 * rows, LANES), jnp.float32),
-            pltpu.VMEM((C, 1, windows), jnp.int32),
-            pltpu.VMEM((R, 1, windows), jnp.int32),
+            pltpu.VMEM((R + C, windows, 2 * rows, LANES), jnp.float32),
+            pltpu.VMEM((R + C, 1, windows), jnp.int32),
             pltpu.VMEM(pair_mask.shape, jnp.int32),
             pltpu.VMEM(table.shape, jnp.float32),
-            DMA((4,)), DMA((R, windows)), DMA((C,)), DMA((2,)), DMA((4,)),
-            REGULAR((R - 1,)), REGULAR((C - 1,)),
+            DMA((R, windows)), DMA((C,)), DMA, DMA((2,)), REGULAR((R - 1,)), REGULAR,
         ],
         compiler_params=pltpu.CompilerParams(collective_id=0, has_side_effects=True),
         name="correlate",

time: 10.5 us -> 10.3 us (0.981)
  Pallas kernels: 9.71 us -> 9.55 us
    pallas_call x1, Pallas kernels: 9.71 us -> 9.55 us  [body(): pl.pallas_call(functools.partial(kernel, R, C), out_shape=pltpu.VMEM((C *...]
where the time goes in v3:
time: 10.3 us; the launch traced here: 10.2 us
  Pallas kernels  9.55 us (93%)
  local copies, waits for them, and re-layouts  0.62 us (6%)
    pallas_call x1, Pallas kernels, body(): pl.pallas_call(functools.partial(kernel, R, C), out_shape=pltpu.VMEM((C *...  9.55 us
    unnamed x1, local copies, waits for them, and re-layouts  0.62 us

profile of v3, /device:TPU:0, one launch (start us, length us, event | category | flops | bytes accessed | tf_op | source)
XLA Modules:
  0.0 10.2 jit_solution(5561569466207170391)
XLA Ops:
  0.0 9.6 %correlate.1 = f32[64,128]{1,0:T(8,128)S(1)} custom-call(f32[1,2,64,128]{3,2,1,0:T(8,128)} %bitcast.16, f32[1,2,64,128]{3,2,1,0:T(8,128)} %bitcast.17, s32[1,2]{1,0:T(1,128)} %zf_hbm.1, s32[1,2]{1,0:T(1,128)} %nf_hbm.1, s32[4,4]{1,0:T(4,128)} %mask_hbm.1, f32[288,128]{1,0:T(8,128)} %constant.2.clone.table_hbm), custom_call_target="tpu_custom_call" | custom-call | tf_op jit(solution)/shard_map/correlate/pallas_call | solution.py:317
  9.6 0.6 %copy.11 = f32[4,4,512]{2,1,0:T(4,128)} copy(f32[4,4,512]{2,1,0:T(4,128)S(1)} %bitcast.15) | data formatting | bytes 65536

commit v4 on v3

--- a/solution.py
+++ b/solution.py
@@ -14,18 +14,16 @@
 MESH = pl.DeviceIdType.MESH
 REACH = 3
 SENDS = (
-    ((0, 1, 3), (0, 3, 5)),
-    ((0, 1, 3), (0, 3, 5)),
-    ((1, 0, 0), (1, 2, 3), (0, 2, 6)),
-    ((1, 0, 0), (1, 2, 3), (2, 0, 6), (0, 2, 6)),
-    ((2, 0, 0), (2, 1, 2), (2, 3, 3), (1, 3, 6)),
-    ((2, 1, 0), (2, 3, 3), (3, 1, 6), (1, 3, 6)),
-    ((3, 0, 0), (3, 1, 2), (3, 2, 2)),
-    ((3, 0, 0), (3, 2, 2)),
+    ((0, 1, (3,)), (0, 3, (5,))),
+    ((0, 1, (3,)), (0, 3, (5,))),
+    ((1, 0, (0,)), (1, 2, (3,)), (0, 2, (6,))),
+    ((1, 0, (0,)), (1, 2, (3,)), (2, 0, (6,)), (0, 2, (6,))),
+    ((2, 0, (0,)), (2, 1, (2,)), (2, 3, (3,)), (1, 3, (6,))),
+    ((2, 1, (0,)), (2, 3, (3,)), (3, 1, (6,)), (1, 3, (6,))),
+    ((3, 0, (0,)), (3, 2, (2,)), (3, 1, (2,))),
+    ((3, 0, (0, 2)), (3, 2, (0,))),
 )
-TAKES = ((1, 2, 3), (1, 2, 3), (0, 2, 3), (0, 2, 3), (1, 3, 0), (1, 3, 0), (2, 0, 1), (2, 0, 1))
-BATCHES = ((0, 1), (2, 3))
-GAIN_AT = 1
+TAKES = ((1, 2, 3), (1, 3, 2), (0, 2, 3), (0, 2, 3), (1, 3, 0), (1, 3, 0), (2, 0, 1), (2, 0, 1))
 
 
 def tables(bins):
@@ -62,8 +60,10 @@
         pltpu.make_async_copy(some, some, sem).wait()
 
     n_load = pltpu.make_async_copy(n_hbm.at[0], held.at[row], n_recv.at[row, 0])
+    n_parts = [pltpu.make_async_copy(n_hbm.at[0, w], held.at[row, w], n_recv.at[row, 0]) for w in range(W)]
     z_load = pltpu.make_async_copy(z_hbm.at[0], held.at[R + col], z_recv.at[col])
-    n_load.start()
+    for part in n_parts:
+        part.start()
     pltpu.make_async_copy(nf_hbm, flags.at[row], sent.at[1]).start()
     pltpu.make_async_copy(zf_hbm, flags.at[R + col], sent.at[1]).start()
     z_load.start()
@@ -119,12 +119,12 @@
     def step_sends(number):
         def send(here):
             for owner, to, when in SENDS[here]:
-                if when == number:
-                    for w in range(W):
+                for w in range(W):
+                    if when[w % len(when)] == number:
                         if owner != here // 2:
                             spectrum(owner, w, to).wait_recv()
                         spectrum(owner, w, to).start()
-        if any(when == number for sends in SENDS for _, _, when in sends):
+        if any(number in when for sends in SENDS for _, _, when in sends):
             at(send)
 
     wait_all(flags, 2, sent.at[1])
@@ -280,18 +280,37 @@
             z_copy(owner, col).wait_recv()
 
     owners = [row] + [pick(p) for p in range(1, R)]
-    done = []
-    for number, batch in enumerate(BATCHES):
-        if number == GAIN_AT:
-            wait_all(flags, R + C - 2, flag_recv)
-            gain = [gains(owner) for owner in owners]
-        for p in batch:
-            if p > 0:
-                receive(p)
-        corrs = [correlate(owners[p]) for p in batch]
-        done += [(p, [[normal(c) for c in part] for part in corr]) for p, corr in zip(batch, corrs)]
-    for p, units in done:
-        finish(owners[p], units, gain[p])
+    gain = []
+
+    def run(batches, keep):
+        done = []
+        for batch in batches:
+            for p in batch:
+                if p > 0:
+                    receive(p)
+            corrs = [correlate(owners[p]) for p in batch]
+            done += [(p, [[normal(c) for c in part] for part in corr]) for p, corr in zip(batch, corrs)]
+            if not gain:
+                wait_all(flags, R + C - 2, flag_recv)
+                gain.extend(gains(owner) for owner in owners)
+            if not keep:
+                for p, units in done:
+                    finish(owners[p], units, gain[p])
+                done = []
+        for p, units in done:
+            finish(owners[p], units, gain[p])
+
+    run([(0, 1)], False)
+    rest = list(range(2, R))
+    together = jnp.logical_not(odd) & (row == 1)
+
+    @pl.when(together)
+    def _():
+        run([rest], True)
+
+    @pl.when(jnp.logical_not(together))
+    def _():
+        run([[p] for p in rest], False)
 
     def finish_sends(here):
         wait_all(held, len(SENDS[here]) + C - 1, sent.at[0])

time: 10.3 us -> 10.1 us (0.981)
  the two profiles are of different devices: /device:TPU:0 before, /device:TPU:1 now
where the time goes in v4:
time: 10.1 us; the launch traced here: 9.95 us
  Pallas kernels  9.32 us (92%)
  local copies, waits for them, and re-layouts  0.62 us (6%)
    pallas_call x1, Pallas kernels, body(): pl.pallas_call(functools.partial(kernel, R, C), out_shape=pltpu.VMEM((C *...  9.32 us
    unnamed x1, local copies, waits for them, and re-layouts  0.62 us

profile of v4, /device:TPU:1, one launch (start us, length us, event | category | flops | bytes accessed | tf_op | source)
XLA Modules:
  0.0 9.9 jit_solution(8648367227439453086)
XLA Ops:
  0.0 9.3 %correlate.1 = f32[64,128]{1,0:T(8,128)S(1)} custom-call(f32[1,2,64,128]{3,2,1,0:T(8,128)} %bitcast.16, f32[1,2,64,128]{3,2,1,0:T(8,128)} %bitcast.17, s32[1,2]{1,0:T(1,128)} %zf_hbm.1, s32[1,2]{1,0:T(1,128)} %nf_hbm.1, s32[4,4]{1,0:T(4,128)} %mask_hbm.1, f32[288,128]{1,0:T(8,128)} %constant.2.clone.table_hbm), custom_call_target="tpu_custom_call" | custom-call | tf_op jit(solution)/shard_map/correlate/pallas_call | solution.py:336
  9.3 0.6 %copy.11 = f32[4,4,512]{2,1,0:T(4,128)} copy(f32[4,4,512]{2,1,0:T(4,128)S(1)} %bitcast.15) | data formatting | bytes 65536

commit v5 on v4

--- a/solution.py
+++ b/solution.py
@@ -14,16 +14,16 @@
 MESH = pl.DeviceIdType.MESH
 REACH = 3
 SENDS = (
-    ((0, 1, (3,)), (0, 3, (5,))),
-    ((0, 1, (3,)), (0, 3, (5,))),
+    ((0, 1, (3,)), (0, 3, (5,)), (2, 1, (8, -1))),
+    ((0, 1, (3,)), (0, 3, (5,)), (2, 1, (7, -1))),
     ((1, 0, (0,)), (1, 2, (3,)), (0, 2, (6,))),
-    ((1, 0, (0,)), (1, 2, (3,)), (2, 0, (6,)), (0, 2, (6,))),
-    ((2, 0, (0,)), (2, 1, (2,)), (2, 3, (3,)), (1, 3, (6,))),
-    ((2, 1, (0,)), (2, 3, (3,)), (3, 1, (6,)), (1, 3, (6,))),
+    ((1, 0, (0,)), (1, 2, (3,)), (2, 0, (-1, 6)), (0, 2, (6,))),
+    ((2, 0, (0,)), (2, 1, (-1, 2)), (2, 3, (3,)), (1, 3, (6,))),
+    ((2, 1, (-1, 0)), (2, 0, (0, -1)), (2, 3, (3,)), (3, 1, (6,)), (1, 3, (6,))),
     ((3, 0, (0,)), (3, 2, (2,)), (3, 1, (2,))),
-    ((3, 0, (0, 2)), (3, 2, (0,))),
+    ((3, 2, (0,)), (3, 0, (2,))),
 )
-TAKES = ((1, 2, 3), (1, 3, 2), (0, 2, 3), (0, 2, 3), (1, 3, 0), (1, 3, 0), (2, 0, 1), (2, 0, 1))
+TAKES = ((1, 2, 3), (1, 2, 3), (0, 2, 3), (0, 2, 3), (1, 3, 0), (1, 3, 0), (2, 0, 1), (2, 0, 1))
 
 
 def tables(bins):
@@ -47,8 +47,8 @@
 def kernel(R, C, z_hbm, n_hbm, zf_hbm, nf_hbm, mask_hbm, table_hbm, out_ref,
            held, flags, mask_buf, table, n_recv, z_recv, flag_recv, sent, row_ready, col_ready):
     row, col = lax.axis_index("row"), lax.axis_index("col")
-    W = held.shape[1]
-    bin_rows = held.shape[2] // 2
+    W = z_hbm.shape[1]
+    bin_rows = held.shape[1] // 2
     period = 2 * bin_rows
     blocks = LAGS // period
     odd = lax.rem(col, 2) == 1
@@ -59,11 +59,17 @@
         some = ref.at[pl.ds(0, count)]
         pltpu.make_async_copy(some, some, sem).wait()
 
-    n_load = pltpu.make_async_copy(n_hbm.at[0], held.at[row], n_recv.at[row, 0])
-    n_parts = [pltpu.make_async_copy(n_hbm.at[0, w], held.at[row, w], n_recv.at[row, 0]) for w in range(W)]
-    z_load = pltpu.make_async_copy(z_hbm.at[0], held.at[R + col], z_recv.at[col])
-    for part in n_parts:
-        part.start()
+    def n_slots(owner):
+        return held.at[pl.ds(owner * W, W)]
+
+    def z_slots(owner):
+        return held.at[pl.ds((R + owner) * W, W)]
+
+    n_load = pltpu.make_async_copy(n_hbm.at[0], n_slots(row), n_recv.at[row, 0])
+    z_load = pltpu.make_async_copy(z_hbm.at[0], z_slots(col), z_recv.at[col])
+    for w in range(W):
+        pltpu.make_async_copy(n_hbm.at[0, w], held.at[row * W + w], n_recv.at[row, 0]).start()
+
     pltpu.make_async_copy(nf_hbm, flags.at[row], sent.at[1]).start()
     pltpu.make_async_copy(zf_hbm, flags.at[R + col], sent.at[1]).start()
     z_load.start()
@@ -98,12 +104,12 @@
 
     def spectrum(owner, w, to):
         return pltpu.make_async_remote_copy(
-            held.at[owner, w], held.at[owner, w], sent.at[0], n_recv.at[owner, w],
+            held.at[owner * W + w], held.at[owner * W + w], sent.at[0], n_recv.at[owner, w],
             device_id={"row": to}, device_id_type=MESH)
 
     def z_copy(owner, to):
         return pltpu.make_async_remote_copy(
-            held.at[R + owner], held.at[R + owner], sent.at[0], z_recv.at[owner],
+            z_slots(owner), z_slots(owner), sent.at[0], z_recv.at[owner],
             device_id={"col": to}, device_id_type=MESH)
 
     def flag(slot, **to):
@@ -218,11 +224,11 @@
         outer = outer.astype(jnp.bfloat16)
         cross = []
         for w in range(W):
-            n_real = held[owner, w, pl.ds(0, bin_rows, stride=2), :] * weight
-            n_imag = held[owner, w, pl.ds(1, bin_rows, stride=2), :] * weight
+            n_real = held[owner * W + w, pl.ds(0, bin_rows, stride=2), :] * weight
+            n_imag = held[owner * W + w, pl.ds(1, bin_rows, stride=2), :] * weight
             for i in range(C):
-                z_real = held[R + i, w, pl.ds(0, bin_rows, stride=2), :]
-                z_imag = held[R + i, w, pl.ds(1, bin_rows, stride=2), :]
+                z_real = held[(R + i) * W + w, pl.ds(0, bin_rows, stride=2), :]
+                z_imag = held[(R + i) * W + w, pl.ds(1, bin_rows, stride=2), :]
                 cross.append(jnp.concatenate(
                     [z_real * n_real + z_imag * n_imag, z_imag * n_real - z_real * n_imag], 0
                 ).astype(jnp.bfloat16))
@@ -267,8 +273,9 @@
     def receive(p):
         def take(here):
             owner = TAKES[here][p - 1]
-            if all(passed != owner for passed, _, _ in SENDS[here]):
-                for w in range(W):
+            passed = [when for passed, _, when in SENDS[here] if passed == owner]
+            for w in range(W):
+                if all(when[w % len(when)] < 0 for when in passed):
                     spectrum(owner, w, here // 2).wait_recv()
         at(take)
 
@@ -280,40 +287,44 @@
             z_copy(owner, col).wait_recv()
 
     owners = [row] + [pick(p) for p in range(1, R)]
-    gain = []
-
-    def run(batches, keep):
-        done = []
-        for batch in batches:
-            for p in batch:
-                if p > 0:
-                    receive(p)
-            corrs = [correlate(owners[p]) for p in batch]
-            done += [(p, [[normal(c) for c in part] for part in corr]) for p, corr in zip(batch, corrs)]
-            if not gain:
+
+    def run(*steps):
+        done, gain = [], []
+        for step in steps:
+            if step == "send":
+                step_sends(R + 4)
+            elif step == "gain":
                 wait_all(flags, R + C - 2, flag_recv)
-                gain.extend(gains(owner) for owner in owners)
-            if not keep:
+                gain = [gains(owner) for owner in owners]
+            else:
+                for p in step:
+                    if p > 0:
+                        receive(p)
+                corrs = [correlate(owners[p]) for p in step]
+                done += [(p, [[normal(c) for c in part] for part in corr]) for p, corr in zip(step, corrs)]
+            if gain:
                 for p, units in done:
                     finish(owners[p], units, gain[p])
                 done = []
-        for p, units in done:
-            finish(owners[p], units, gain[p])
-
-    run([(0, 1)], False)
-    rest = list(range(2, R))
+
+    alone = jnp.logical_not(odd) & (row == 0)
     together = jnp.logical_not(odd) & (row == 1)
 
+    @pl.when(alone)
+    def _():
+        run([0], "send", [1], "gain", [2], [3])
+
     @pl.when(together)
     def _():
-        run([rest], True)
-
-    @pl.when(jnp.logical_not(together))
-    def _():
-        run([[p] for p in rest], False)
+        run([0, 1], "send", "gain", [2, 3])
+
+    @pl.when(jnp.logical_not(alone | together))
+    def _():
+        run([0, 1], "send", "gain", [2], [3])
 
     def finish_sends(here):
-        wait_all(held, len(SENDS[here]) + C - 1, sent.at[0])
+        windows = sum(when[w % len(when)] >= 0 for _, _, when in SENDS[here] for w in range(W))
+        wait_all(held, windows + (C - 1) * W, sent.at[0])
 
     at(finish_sends)
     wait_all(flags, R + C - 2, sent.at[1])
@@ -339,7 +350,7 @@
         in_specs=[pl.BlockSpec(memory_space=pl.ANY)] * 6,
         out_specs=pl.BlockSpec(memory_space=pltpu.VMEM),
         scratch_shapes=[
-            pltpu.VMEM((R + C, windows, 2 * rows, LANES), jnp.float32),
+            pltpu.VMEM(((R + C) * windows, 2 * rows, LANES), jnp.float32),
             pltpu.VMEM((R + C, 1, windows), jnp.int32),
             pltpu.VMEM(pair_mask.shape, jnp.int32),
             pltpu.VMEM(table.shape, jnp.float32),

time: 10.1 us -> 9.91 us (0.981)
  Pallas kernels: 9.32 us -> 9.13 us
    pallas_call x1, Pallas kernels: 9.32 us -> 9.13 us  [body(): pl.pallas_call(functools.partial(kernel, R, C), out_shape=pltpu.VMEM((C *...]
where the time goes in v5:
time: 9.91 us; the launch traced here: 9.75 us
  Pallas kernels  9.13 us (92%)
  local copies, waits for them, and re-layouts  0.62 us (6%)
    pallas_call x1, Pallas kernels, body(): pl.pallas_call(functools.partial(kernel, R, C), out_shape=pltpu.VMEM((C *...  9.13 us
    unnamed x1, local copies, waits for them, and re-layouts  0.62 us

profile of v5, /device:TPU:1, one launch (start us, length us, event | category | flops | bytes accessed | tf_op | source)
XLA Modules:
  0.0 9.8 jit_solution(5773016108924467147)
XLA Ops:
  0.0 9.1 %correlate.1 = f32[64,128]{1,0:T(8,128)S(1)} custom-call(f32[1,2,64,128]{3,2,1,0:T(8,128)} %bitcast.16, f32[1,2,64,128]{3,2,1,0:T(8,128)} %bitcast.17, s32[1,2]{1,0:T(1,128)} %zf_hbm.1, s32[1,2]{1,0:T(1,128)} %nf_hbm.1, s32[4,4]{1,0:T(4,128)} %mask_hbm.1, f32[288,128]{1,0:T(8,128)} %constant.2.clone.table_hbm), custom_call_target="tpu_custom_call" | custom-call | tf_op jit(solution)/shard_map/correlate/pallas_call | solution.py:347
  9.1 0.6 %copy.11 = f32[4,4,512]{2,1,0:T(4,128)} copy(f32[4,4,512]{2,1,0:T(4,128)S(1)} %bitcast.15) | data formatting | bytes 65536
